TPU v7x, 32 devices: a whole 2x2x4 slice. The times are simulated.
32 devices in a mesh: grp: 2 (over y), blk: 8 (over z, x), uly: 2 (over core).
Axes of the slice: x: 2, y: 2, z: 4, core: 2. Of those that a mesh axis runs over, the one named last changes fastest.
Arguments:
- query: bfloat16 [512, 1152], P(('grp', 'blk', 'uly')), parts along dimension 0, may hold values from -6 to 6
- key: bfloat16 [512, 1152], P(('grp', 'blk', 'uly')), parts along dimension 0, may hold values from -6 to 6
- value: bfloat16 [512, 1152], P(('grp', 'blk', 'uly')), parts along dimension 0, may hold values from -6 to 6
- q_gain: float32 [96], replicated, may hold values from 1 to 2.5
- k_gain: float32 [96], replicated, may hold values from 1 to 2.5
- out_weight: bfloat16 [1152, 2304], P('uly'), may hold values from -0.1875 to 0.1875
Outputs:
- mixed: bfloat16 [512, 2304], P(('grp', 'blk', 'uly')), parts along dimension 0
There are 2 independent parts, one for each index of `grp`. A program takes and returns all parts, laid end to end along the dimension named above; an argument that names none is the same for every part. Nothing has to cross between parts.
All inputs are finite; a program needn't handle non-finite values.
Results may differ from a plain program's by a relative error of at most 0.012.
Values may be sent and summed in bfloat16 or wider, within the bound.
No kernel may reach another device: no remote copies, remote signals or barrier semaphores. Data moves between devices by JAX's collectives and lax.ppermute only.
A program may use at most 128 MiB of HBM per device.

v0:
```python
import jax
import jax.numpy as jnp
from jax import lax
from jax.sharding import PartitionSpec as P

H = 12
HD = 96


def partner_2(block, axis, apart):
    count = lax.axis_size(axis)
    route = []
    for low in range(count):
        high = low | 1 << apart
        if high != low and high < count:
            route += [(low, high), (high, low)]
    return lax.ppermute(block, axis, route)


def from_behind(value, axis, steps):
    count = lax.axis_size(axis)
    pairs = [(source, (source + steps) % count) for source in range(count)]
    return lax.ppermute(value, axis, pairs)


def normed(data, gain):
    tok_rows = data.shape[0]
    grid = data.astype(jnp.float32).reshape(tok_rows, H, HD)
    meansq = jnp.mean(grid * grid, axis=-1, keepdims=True)
    return (grid * lax.rsqrt(meansq + 1e-06) * gain).astype(jnp.bfloat16).reshape(tok_rows, H * HD)


def attend_block(query_heads, carry, kv_piece):
    weighted, total_weight = carry
    length = kv_piece.shape[1]
    head_count = query_heads.shape[1]
    key_heads = kv_piece[0].reshape(length, head_count, HD)
    value_heads = kv_piece[1].reshape(length, head_count, HD)
    score_scale = float(HD) ** (-0.5)
    scores = (
        jnp.einsum("qhd,khd->hqk", query_heads, key_heads, preferred_element_type=jnp.float32)
        * score_scale
    )
    expd = jnp.exp(scores)
    total_weight = total_weight + jnp.sum(expd, axis=-1).T
    weighted = weighted + jnp.einsum(
        "hqk,khd->qhd", expd.astype(jnp.bfloat16), value_heads, preferred_element_type=jnp.float32
    )
    return (weighted, total_weight)


def on_device(query, key, value, q_gain, k_gain, out_weight):
    query_normed = normed(query, q_gain)
    key_normed = normed(key, k_gain)
    query_group, key_group, value_group = (
        lax.all_to_all(query_normed, "uly", split_axis=1, concat_axis=0, tiled=True),
        lax.all_to_all(key_normed, "uly", split_axis=1, concat_axis=0, tiled=True),
        lax.all_to_all(value, "uly", split_axis=1, concat_axis=0, tiled=True),
    )
    row_count = query_group.shape[0]
    local_heads = query_group.shape[1] // HD
    half_heads = local_heads // 2
    half_width = half_heads * HD
    parity = lax.axis_index("blk") % 2
    stacked = jnp.stack([query_group, key_group, value_group])
    mine = lax.dynamic_slice_in_dim(stacked, parity * half_width, half_width, 2)
    others = lax.dynamic_slice_in_dim(stacked, (1 - parity) * half_width, half_width, 2)
    partner = partner_2(others, "blk", 0)
    paired = jnp.where(
        parity == 0, jnp.concatenate([mine, partner], 1), jnp.concatenate([partner, mine], 1)
    )
    pair_rows = 2 * row_count
    query_heads = paired[0].reshape(pair_rows, half_heads, HD)
    gathered = paired[1:3]
    members = lax.axis_size("blk") // 2
    held = 1
    while held < members:
        take = min(held, members - held)
        arrived = from_behind(gathered, "blk", 2 * held)
        gathered = jnp.concatenate([gathered, arrived], 1)
        held = held + take
    group_size = 1
    for factor in range(1, members + 1):
        if members % factor == 0 and factor * pair_rows <= 1024:
            group_size = factor
    block_rows = group_size * pair_rows
    block_count = members // group_size
    blocks = jnp.transpose(gathered.reshape(2, block_count, block_rows, half_width), (1, 0, 2, 3))

    def scan_step(carry, kv_piece):
        return (attend_block(query_heads, carry, kv_piece), None)

    start_carry = (
        jnp.zeros((pair_rows, half_heads, HD), jnp.float32),
        jnp.zeros((pair_rows, half_heads), jnp.float32),
    )
    (weighted, total_weight), unused = lax.scan(scan_step, start_carry, blocks)
    attn_pair = (
        (weighted / total_weight[:, :, None]).astype(jnp.bfloat16).reshape(pair_rows, half_width)
    )
    own_rows = lax.dynamic_slice_in_dim(attn_pair, parity * row_count, row_count, 0)
    send_rows = lax.dynamic_slice_in_dim(attn_pair, (1 - parity) * row_count, row_count, 0)
    returned = partner_2(send_rows, "blk", 0)
    attn = jnp.where(
        parity == 0,
        jnp.concatenate([own_rows, returned], 1),
        jnp.concatenate([returned, own_rows], 1),
    )
    attn_tokens = lax.all_to_all(attn, "uly", split_axis=0, concat_axis=1, tiled=True)
    mixed = jnp.dot(
        attn_tokens,
        lax.all_gather(out_weight, "uly", axis=0, tiled=True),
        preferred_element_type=jnp.float32,
    )
    return mixed.astype(jnp.bfloat16)


def solution(mesh):
    in_specs = (
        P(("grp", "blk", "uly"), None),
        P(("grp", "blk", "uly"), None),
        P(("grp", "blk", "uly"), None),
        P(),
        P(),
        P("uly", None),
    )
    out_specs = P(("grp", "blk", "uly"), None)
    return jax.shard_map(
        on_device, mesh=mesh, in_specs=in_specs, out_specs=out_specs, check_vma=False
    )
```

profile of v0, /device:TPU:0, one launch (start us, length us, event | category | flops | bytes accessed | tf_op | source)
XLA Modules:
  0.0 66.7 jit_solution(3177109753742246567)
XLA Ops:
  6.5 0.0 all-gather.2.cloned.1.call-start
  6.5 0.7 %all-gather.2.cloned.1.call-update = ((bf16[576,2304]{1,0:T(8,128)(2,1)}), bf16[1152,2304]{1,0:T(8,128)(2,1)}) async-update(((), (), s32[]{:S(2)}) %all-gather.2.cloned.1.call-start, bf16[576,2304]{1,0:T(8,128)(2,1)} %param.11) | async-update | bytes 10616856
  7.3 0.8 %convert_multiply_fusion.3 = f32[16,1152]{1,0:T(8,128)S(1)} fusion(bf16[16,1152]{1,0:T(8,128)(2,1)} %param.6), kind=kLoop, calls=%fused_computation.14 | loop fusion | flops 36864 | bytes 110592 | tf_op jit(solution)/shard_map/mul | solution.py:29
  8.0 0.1 mul.77
  8.1 0.1 reduce_sum.28
  8.3 0.1 mul.78
  8.4 0.1 mul.79
  8.5 0.7 mul.81
  9.1 0.1 mul.82
  9.2 0.8 %fusion.5 = bf16[16,1152]{1,0:T(8,128)(2,1)S(1)} fusion(f32[16,1152]{1,0:T(8,128)S(1)} %mul.79, bf16[16,1152]{1,0:T(8,128)(2,1)} %param.6, f32[1152]{0:T(1024)S(1)} %mul.82), kind=kLoop, calls=%fused_computation.16 | loop fusion | flops 73728 | bytes 152064 | tf_op jit(solution)/shard_map/convert_element_type | solution.py:30
  10.0 0.1 all_to_all.48
  10.1 0.6 copy.26
  10.7 3.3 %all-to-all-start = ((bf16[16,2,576]{2,0,1:T(8,128)(2,1)}), bf16[16,2,576]{2,0,1:T(8,128)(2,1)S(1)}, u32[]{:S(2)}, u32[]{:S(2)}) async-start(bf16[16,2,576]{2,0,1:T(8,128)(2,1)} %copy.26), calls=%async_computation | async-start | bytes 81920 | tf_op jit(solution)/shard_map/all_to_all | solution.py:56
  14.0 0.8 %convert_multiply_fusion.1 = f32[16,1152]{1,0:T(8,128)S(1)} fusion(bf16[16,1152]{1,0:T(8,128)(2,1)} %param.7), kind=kLoop, calls=%fused_computation.12 | loop fusion | flops 36864 | bytes 110592 | tf_op jit(solution)/shard_map/mul | solution.py:29
  14.8 0.1 mul.86
  14.9 0.1 reduce_sum.29
  15.0 0.1 mul.87
  15.1 0.1 mul.88
  15.2 0.7 mul.90
  15.9 0.1 mul.91
  16.0 0.8 %fusion.7 = bf16[16,1152]{1,0:T(8,128)(2,1)S(1)} fusion(f32[16,1152]{1,0:T(8,128)S(1)} %mul.88, bf16[16,1152]{1,0:T(8,128)(2,1)} %param.7, f32[1152]{0:T(1024)S(1)} %mul.91), kind=kLoop, calls=%fused_computation.18 | loop fusion | flops 73728 | bytes 152064 | tf_op jit(solution)/shard_map/convert_element_type | solution.py:30
  16.8 0.1 all_to_all.51
  16.9 0.9 %all_to_all.54 = bf16[16,2,576]{2,1,0:T(2,128)(2,1)S(1)} reshape(bf16[16,1152]{1,0:T(8,128)(2,1)} %param.8) | data formatting | bytes 73728 | tf_op jit(solution)/shard_map/all_to_all | solution.py:58
  17.8 0.0 all-to-all-done
  17.8 3.8 %all_to_all.64 = bf16[16,2,576]{2,0,1:T(8,128)(2,1)S(1)} all-to-all(bf16[16,2,576]{2,0,1:T(8,128)(2,1)S(1)} %copy.27), channel_id=1, replica_groups=mesh['grp'=2,'blk'=8,'uly'=2] {'uly'}, dimensions={1} | all-to-all | bytes 73728 | tf_op jit(solution)/shard_map/all_to_all | solution.py:57
  21.6 3.8 %all_to_all.65 = bf16[16,2,576]{2,0,1:T(8,128)(2,1)S(1)} all-to-all(bf16[16,2,576]{2,0,1:T(8,128)(2,1)S(1)} %copy.28), channel_id=1, replica_groups=mesh['grp'=2,'blk'=8,'uly'=2] {'uly'}, dimensions={1} | all-to-all | bytes 73728 | tf_op jit(solution)/shard_map/all_to_all | solution.py:58
  25.4 0.1 constant_dynamic-slice_fusion.3
  25.5 3.0 %collective-permute-start = (bf16[3,32,288]{2,1,0:T(8,128)(2,1)S(1)}, bf16[3,32,288]{2,1,0:T(8,128)(2,1)S(1)}, u32[]{:S(2)}, u32[]{:S(2)}) collective-permute-start(bf16[3,32,288]{2,1,0:T(8,128)(2,1)S(1)} %get-tuple-element.22), channel_id=1, source_target_pairs={{0,2},{2,0},{4,6},{6,4},{8,10},{10,8},{12,14},{14,12},{1,3},{3,1},... | collective-permute-start | bytes 165896 | tf_op jit(solution)/shard_map/ppermute | solution.py:17
  28.6 2.6 %collective-permute-done = bf16[3,32,288]{2,1,0:T(8,128)(2,1)S(1)} collective-permute-done((bf16[3,32,288]{2,1,0:T(8,128)(2,1)S(1)}, bf16[3,32,288]{2,1,0:T(8,128)(2,1)S(1)}, u32[]{:S(2)}, u32[]{:S(2)}) %collective-permute-start) | collective-permute-done | bytes 55328 | tf_op jit(solution)/shard_map/ppermute | solution.py:17
  31.2 1.9 %collective-permute-start.1 = (bf16[2,64,288]{2,1,0:T(8,128)(2,1)S(1)}, bf16[2,64,288]{2,1,0:T(8,128)(2,1)S(1)}, u32[]{:S(2)}, u32[]{:S(2)}) collective-permute-start(bf16[2,64,288]{2,1,0:T(8,128)(2,1)S(1)} %slice.19), channel_id=1, source_target_pairs={{0,4},{2,6},{4,8},{6,10},{8,12},{10,14},{12,0},{14,2},{1,5},{3,7},... | collective-permute-start | bytes 221192 | tf_op jit(solution)/shard_map/ppermute | solution.py:23
  33.1 4.6 %collective-permute-done.1 = bf16[2,64,288]{2,1,0:T(8,128)(2,1)S(1)} collective-permute-done((bf16[2,64,288]{2,1,0:T(8,128)(2,1)S(1)}, bf16[2,64,288]{2,1,0:T(8,128)(2,1)S(1)}, u32[]{:S(2)}, u32[]{:S(2)}) %collective-permute-start.1) | collective-permute-done | bytes 73760 | tf_op jit(solution)/shard_map/ppermute | solution.py:23
  37.7 1.1 %collective-permute-start.2 = (bf16[2,128,288]{2,1,0:T(8,128)(2,1)S(1)}, bf16[2,128,288]{2,1,0:T(8,128)(2,1)S(1)}, u32[]{:S(2)}, u32[]{:S(2)}) collective-permute-start(bf16[2,128,288]{2,1,0:T(8,128)(2,1)S(1)} %pad_maximum_fusion.1), channel_id=1, source_target_pairs={{0,8},{2,10},{4,12},{6,14},{8,0},{10,2},{12,4},{14,6},{1,9},{3,11}... | collective-permute-start | bytes 442376 | tf_op jit(solution)/shard_map/ppermute | solution.py:23
  38.8 0.1 reshape_squeeze.3
  38.9 8.1 %collective-permute-done.2 = bf16[2,128,288]{2,1,0:T(8,128)(2,1)S(1)} collective-permute-done((bf16[2,128,288]{2,1,0:T(8,128)(2,1)S(1)}, bf16[2,128,288]{2,1,0:T(8,128)(2,1)S(1)}, u32[]{:S(2)}, u32[]{:S(2)}) %collective-permute-start.2) | collective-permute-done | bytes 147488 | tf_op jit(solution)/shard_map/ppermute | solution.py:23
  47.1 0.1 copy.30
  47.2 0.1 copy.29
  47.4 0.3 fusion.10
  47.6 0.2 fusion.2
  47.9 0.1 reshape.55
  48.0 1.6 %collective-permute-start.3 = (bf16[32,288]{1,0:T(8,128)(2,1)S(1)}, bf16[32,288]{1,0:T(8,128)(2,1)S(1)}, u32[]{:S(2)}, u32[]{:S(2)}) collective-permute-start(bf16[32,288]{1,0:T(8,128)(2,1)S(1)} %get-tuple-element.25), channel_id=1, source_target_pairs={{0,2},{2,0},{4,6},{6,4},{8,10},{10,8},{12,14},{14,12},{1,3},{3,1},... | collective-permute-start | bytes 55304 | tf_op jit(solution)/shard_map/ppermute | solution.py:17
  49.5 2.3 %collective-permute-done.3 = bf16[32,288]{1,0:T(8,128)(2,1)S(1)} collective-permute-done((bf16[32,288]{1,0:T(8,128)(2,1)S(1)}, bf16[32,288]{1,0:T(8,128)(2,1)S(1)}, u32[]{:S(2)}, u32[]{:S(2)}) %collective-permute-start.3) | collective-permute-done | bytes 18464 | tf_op jit(solution)/shard_map/ppermute | solution.py:17
  51.9 0.1 maximum_select_fusion.1
  52.0 3.8 %all_to_all.66 = bf16[2,16,576]{2,1,0:T(8,128)(2,1)S(1)} all-to-all(bf16[2,16,576]{2,1,0:T(8,128)(2,1)S(1)} %maximum_select_fusion.1), channel_id=1, replica_groups=mesh['grp'=2,'blk'=8,'uly'=2] {'uly'}, dimensions={0} | all-to-all | bytes 73728 | tf_op jit(solution)/shard_map/all_to_all | solution.py:109
  55.8 0.1 all_to_all.59
  55.9 0.0 all-gather.2.cloned.1.call-done
  55.9 4.0 %convolution_convert_fusion = bf16[16,2304]{1,0:T(8,128)(2,1)} fusion(bf16[16,1152]{1,0:T(8,128)(2,1)S(1)} %all_to_all.59, bf16[1152,2304]{1,0:T(8,128)(2,1)} %all-gather.2.cloned.1.call-done), kind=kOutput, calls=%fused_computation | convolution fusion | flops 84971520 | bytes 5419008 | tf_op jit(solution)/shard_map/dot_general | solution.py:110
  (14 shorter events, 0.3 us)
Async XLA Ops:
  6.5 49.4 %all-gather.2.cloned.1.call-start = ((), (), s32[]{:S(2)}) async-start(), calls=%async_computation.4 | async-start | bytes 7962624 | tf_op jit(solution)/shard_map/all_gather | solution.py:112
  10.7 7.1 %all-to-all-start = ((bf16[16,2,576]{2,0,1:T(8,128)(2,1)}), bf16[16,2,576]{2,0,1:T(8,128)(2,1)S(1)}, u32[]{:S(2)}, u32[]{:S(2)}) async-start(bf16[16,2,576]{2,0,1:T(8,128)(2,1)} %copy.26), calls=%async_computation | async-start | bytes 81920 | tf_op jit(solution)/shard_map/all_to_all | solution.py:56
  25.5 5.6 %collective-permute-start = (bf16[3,32,288]{2,1,0:T(8,128)(2,1)S(1)}, bf16[3,32,288]{2,1,0:T(8,128)(2,1)S(1)}, u32[]{:S(2)}, u32[]{:S(2)}) collective-permute-start(bf16[3,32,288]{2,1,0:T(8,128)(2,1)S(1)} %get-tuple-element.22), channel_id=1, source_target_pairs={{0,2},{2,0},{4,6},{6,4},{8,10},{10,8},{12,14},{14,12},{1,3},{3,1},... | collective-permute-start | bytes 165896 | tf_op jit(solution)/shard_map/ppermute | solution.py:17
  31.2 6.5 %collective-permute-start.1 = (bf16[2,64,288]{2,1,0:T(8,128)(2,1)S(1)}, bf16[2,64,288]{2,1,0:T(8,128)(2,1)S(1)}, u32[]{:S(2)}, u32[]{:S(2)}) collective-permute-start(bf16[2,64,288]{2,1,0:T(8,128)(2,1)S(1)} %slice.19), channel_id=1, source_target_pairs={{0,4},{2,6},{4,8},{6,10},{8,12},{10,14},{12,0},{14,2},{1,5},{3,7},... | collective-permute-start | bytes 221192 | tf_op jit(solution)/shard_map/ppermute | solution.py:23
  37.7 9.3 %collective-permute-start.2 = (bf16[2,128,288]{2,1,0:T(8,128)(2,1)S(1)}, bf16[2,128,288]{2,1,0:T(8,128)(2,1)S(1)}, u32[]{:S(2)}, u32[]{:S(2)}) collective-permute-start(bf16[2,128,288]{2,1,0:T(8,128)(2,1)S(1)} %pad_maximum_fusion.1), channel_id=1, source_target_pairs={{0,8},{2,10},{4,12},{6,14},{8,0},{10,2},{12,4},{14,6},{1,9},{3,11}... | collective-permute-start | bytes 442376 | tf_op jit(solution)/shard_map/ppermute | solution.py:23
  48.0 3.9 %collective-permute-start.3 = (bf16[32,288]{1,0:T(8,128)(2,1)S(1)}, bf16[32,288]{1,0:T(8,128)(2,1)S(1)}, u32[]{:S(2)}, u32[]{:S(2)}) collective-permute-start(bf16[32,288]{1,0:T(8,128)(2,1)S(1)} %get-tuple-element.25), channel_id=1, source_target_pairs={{0,2},{2,0},{4,6},{6,4},{8,10},{10,8},{12,14},{14,12},{1,3},{3,1},... | collective-permute-start | bytes 55304 | tf_op jit(solution)/shard_map/ppermute | solution.py:17
Sparse Core Ops, SparseCore 0:
  8.9 18.0 all-gather.1
where the time goes:
time: 67.4 us; the launch traced here: 66.7 us
  waiting for transfers between devices  18.3 us (27%)
  between operations  13.6 us (20%)
  blocking collectives  11.3 us (17%)
  starting transfers between devices  10.9 us (16%)
  local copies, waits for them, and re-layouts  4.6 us (7%)
  matrix products  4.39 us (7%)
  other arithmetic  3.56 us (5%)
    ppermute x2, waiting for transfers between devices, from_behind(): return lax.ppermute(value, axis, pairs)  12.7 us
    ppermute x2, waiting for transfers between devices, partner_2(): return lax.ppermute(block, axis, route)  4.91 us
    ppermute x2, starting transfers between devices, partner_2(): return lax.ppermute(block, axis, route)  4.59 us
    dot_general x1, matrix products, on_device(): jnp.dot(attn_tokens, lax.all_gather(out_weight, 'uly', axis=0, tiled=True...  3.96 us
    all_to_all x1, blocking collectives, on_device(): lax.all_to_all(value, 'uly', split_axis=1, concat_axis=0, tiled=True)  3.78 us
    all_to_all x1, blocking collectives, on_device(): lax.all_to_all(attn, 'uly', split_axis=0, concat_axis=1, tiled=True)  3.76 us
    all_to_all x1, blocking collectives, on_device(): lax.all_to_all(key_normed, 'uly', split_axis=1, concat_axis=0, tiled=True)  3.76 us
    all_to_all x1, starting transfers between devices, on_device(): lax.all_to_all(query_normed, 'uly', split_axis=1, concat_axis=0, tiled=True)  3.27 us
  transfers between devices with their start and end apart: 6, of which 4 were waited for; matrix products, arithmetic and copies ran while one was open for 11% of the time, Pallas kernels for 0%

commit v1 on v0

v1 whole, which is shorter than its diff:
```python
import jax
import jax.numpy as jnp
from jax import lax
from jax.experimental import pallas as pl
from jax.experimental.pallas import tpu as pltpu
from jax.sharding import PartitionSpec as P

H = 12
HD = 96
DIRECT = 8


def swap(block, axis, mask):
    count = lax.axis_size(axis)
    return lax.ppermute(block, axis, [(i, i ^ mask) for i in range(count)])


def head_of(rows, width):
    lane = lax.broadcasted_iota(jnp.int32, (rows, width), 1)
    first = lax.broadcasted_iota(jnp.int32, (rows, width), 0) * HD
    return (lane >= first) & (lane < first + HD)


def lane_of(width, cols):
    lane = lax.broadcasted_iota(jnp.int32, (width, cols), 0)
    first = lax.broadcasted_iota(jnp.int32, (width, cols), 1) * HD
    return (lane >= first) & (lane < first + HD)


def pieces(value, count):
    out = []
    for _ in range(count):
        part = value.astype(jnp.bfloat16)
        out.append(part)
        value = value - part.astype(jnp.float32)
    return out


def dot(a, b):
    return jnp.dot(a, b, preferred_element_type=jnp.float32)


def normed_rows(data, gain, gather, spread):
    grid = data.astype(jnp.float32)
    square = sum(dot(part, gather) for part in pieces(grid * grid, 2))
    inverse = lax.rsqrt(square * (1.0 / HD) + 1e-06)
    wide = sum(dot(part, spread) for part in pieces(inverse, 3))
    return (grid * wide * gain).astype(jnp.bfloat16)


def attend_kernel(q_ref, mine_ref, theirs_ref, gain_ref, out_ref):
    rows, width = q_ref.shape
    gather = lane_of(width, 128).astype(jnp.bfloat16)
    spread = head_of(128, width).astype(jnp.bfloat16)
    key = jnp.concatenate([mine_ref[:, :width], theirs_ref[:, :width]], 0)
    value = jnp.concatenate([mine_ref[:, width:], theirs_ref[:, width:]], 0)
    query_n = normed_rows(q_ref[...], gain_ref[0:1, :], gather, spread)
    key_n = normed_rows(key, gain_ref[1:2, :], gather, spread)
    lane = lax.broadcasted_iota(jnp.int32, (rows, width), 1)
    masks = [(lane >= h * HD) & (lane < (h + 1) * HD) for h in range(H)]
    query_f = query_n.astype(jnp.float32)
    stacked = jnp.concatenate([jnp.where(m, query_f, 0.0) for m in masks], 0).astype(jnp.bfloat16)
    scores = lax.dot_general(
        stacked, key_n, (((1,), (1,)), ((), ())), preferred_element_type=jnp.float32
    ) * (float(HD) ** (-0.5))
    expd = jnp.exp(scores)
    total = jnp.sum(expd, axis=1, keepdims=True)
    weighted = dot(expd.astype(jnp.bfloat16), value)
    top = jnp.zeros((rows, width), jnp.float32)
    below = jnp.zeros((rows, width), jnp.float32)
    for h in range(H):
        top = jnp.where(masks[h], weighted[h * rows : (h + 1) * rows], top)
        below = jnp.where(masks[h], total[h * rows : (h + 1) * rows], below)
    out_ref[...] = (top / below).astype(out_ref.dtype)


def normed(data, gain):
    tok_rows = data.shape[0]
    grid = data.astype(jnp.float32).reshape(tok_rows, H, HD)
    meansq = jnp.mean(grid * grid, axis=-1, keepdims=True)
    return (grid * lax.rsqrt(meansq + 1e-06) * gain).astype(jnp.bfloat16)


def general(query, key, value, q_gain, k_gain, out_weight):
    rows, width = query.shape
    keys = lax.all_gather(normed(key, k_gain).reshape(rows, width), ("blk", "uly"), axis=0, tiled=True)
    values = lax.all_gather(value, ("blk", "uly"), axis=0, tiled=True)
    keys, values = keys.reshape(-1, H, HD), values.reshape(-1, H, HD)
    scores = jnp.einsum("qhd,khd->hqk", normed(query, q_gain), keys, preferred_element_type=jnp.float32)
    expd = jnp.exp(scores * (float(HD) ** (-0.5)))
    total = jnp.sum(expd, axis=-1).T
    weighted = jnp.einsum(
        "hqk,khd->qhd", expd.astype(jnp.bfloat16), values, preferred_element_type=jnp.float32
    )
    attn = (weighted / total[:, :, None]).astype(jnp.bfloat16).reshape(rows, width)
    weight = lax.all_gather(out_weight, "uly", axis=0, tiled=True)
    return dot(attn, weight).astype(jnp.bfloat16)


def direct(query, key, value, q_gain, k_gain, out_weight):
    rows, width = query.shape
    blocks = lax.axis_size("blk")
    other_weight = swap(out_weight, "uly", 1)
    held = [jnp.concatenate([key, value], 1)]
    held += [swap(held[0], "blk", mask) for mask in range(2, blocks, 2)]
    held += [swap(block, "blk", 1) for block in held]
    mine = jnp.concatenate(held, 0)
    theirs = swap(mine, "uly", 1)
    gains = jnp.stack([jnp.tile(q_gain, H), jnp.tile(k_gain, H)])
    attn = pl.pallas_call(
        attend_kernel,
        out_shape=jax.ShapeDtypeStruct((rows, width), jnp.bfloat16),
        in_specs=[pl.BlockSpec(memory_space=pltpu.VMEM)] * 4,
        out_specs=pl.BlockSpec(memory_space=pltpu.VMEM),
    )(query, mine, theirs, gains)
    half = width // 2
    first = lax.axis_index("uly") == 0
    own = jnp.where(first, attn[:, :half], attn[:, half:])
    other = jnp.where(first, attn[:, half:], attn[:, :half])
    return (dot(own, out_weight) + dot(other, other_weight)).astype(jnp.bfloat16)


def solution(mesh):
    blocks = mesh.shape["blk"]
    small = mesh.shape["uly"] == 2 and 1 < blocks <= DIRECT and blocks & (blocks - 1) == 0
    rows = P(("grp", "blk", "uly"), None)
    return jax.shard_map(
        direct if small else general,
        mesh=mesh,
        in_specs=(rows, rows, rows, P(), P(), P("uly", None)),
        out_specs=rows,
        check_vma=False,
    )
```

time: 67.4 us -> 29 us (0.43)
  between operations: 13.6 us -> 0.1 us
  waiting for transfers between devices: 18.3 us -> 5.82 us
  blocking collectives: 11.3 us -> 0 us
  Pallas kernels: 0 us -> 4.1 us
  other arithmetic: 3.56 us -> 0.61 us
  local copies, waits for them, and re-layouts: 4.6 us -> 3.28 us
  matrix products: 4.39 us -> 3.44 us
    ppermute x4 -> x9, waiting for transfers between devices: 17.6 us -> 5.82 us  [swap(): return lax.ppermute(block, axis, [(i, i ^ mask) for i in range(count)])]
    all_to_all x3 -> x0, blocking collectives: 11.3 us -> none  [the longest x1 3.78 us: on_device(): lax.all_to_all(value, 'uly', split_axis=1, concat_axis=0, tiled=True)]
    pallas_call x0 -> x1, Pallas kernels: none -> 4.1 us  [direct(): pl.pallas_call(attend_kernel, out_shape=jax.ShapeDtypeStruct((rows, width...]
    ppermute x4 -> x9, starting transfers between devices: 7.62 us -> 11.3 us  [swap(): return lax.ppermute(block, axis, [(i, i ^ mask) for i in range(count)])]
    all_to_all x1 -> x0, starting transfers between devices: 3.27 us -> none  [on_device(): lax.all_to_all(query_normed, 'uly', split_axis=1, concat_axis=0, tiled=True)]
    mul x10 -> x0, local copies, waits for them, and re-layouts: 2.05 us -> none  [the longest x8 1.84 us: normed(): grid * lax.rsqrt(meansq + 1e-06) * gain]
    all_to_all x8 -> x0, local copies, waits for them, and re-layouts: 1.88 us -> none  [the longest x2 0.89 us: on_device(): lax.all_to_all(value, 'uly', split_axis=1, concat_axis=0, tiled=True)]
    convert_element_type x2 -> x0, other arithmetic: 1.56 us -> none  [normed(): (grid * lax.rsqrt(meansq + 1e-06) * gain).astype(jnp.bfloat16)]
  transfers between devices with their start and end apart: 6 -> 9, of which waited for: 4 -> 3; matrix products, arithmetic and copies ran while one was open for 11% -> 8% of each run, Pallas kernels for 0% -> 14%
where the time goes in v1:
time: 29 us; the launch traced here: 28.7 us
  starting transfers between devices  11.3 us (39%)
  waiting for transfers between devices  5.82 us (20%)
  Pallas kernels  4.1 us (14%)
  matrix products  3.44 us (12%)
  local copies, waits for them, and re-layouts  3.28 us (11%)
  other arithmetic  0.61 us (2%)
    ppermute x9, starting transfers between devices, swap(): return lax.ppermute(block, axis, [(i, i ^ mask) for i in range(count)])  11.3 us
    ppermute x9, waiting for transfers between devices, swap(): return lax.ppermute(block, axis, [(i, i ^ mask) for i in range(count)])  5.82 us
    pallas_call x1, Pallas kernels, direct(): pl.pallas_call(attend_kernel, out_shape=jax.ShapeDtypeStruct((rows, width...  4.1 us
    dot_general x2, matrix products, dot(): return jnp.dot(a, b, preferred_element_type=jnp.float32)  3.44 us
    another operation x4, local copies, waits for them, and re-layouts, direct(): gains = jnp.stack([jnp.tile(q_gain, H), jnp.tile(k_gain, H)])  1.52 us
    concatenate x1, local copies, waits for them, and re-layouts, direct(): held = [jnp.concatenate([key, value], 1)]  0.93 us
    unnamed x13, local copies, waits for them, and re-layouts  0.82 us
    another operation x1, other arithmetic, direct(): gains = jnp.stack([jnp.tile(q_gain, H), jnp.tile(k_gain, H)])  0.61 us
  transfers between devices with their start and end apart: 9, of which 3 were waited for; matrix products, arithmetic and copies ran while one was open for 8% of the time, Pallas kernels for 14%

profile of v1, /device:TPU:0, one launch (start us, length us, event | category | flops | bytes accessed | tf_op | source)
XLA Modules:
  0.0 28.7 jit_solution(10270768565032195887)
XLA Ops:
  0.0 0.8 %constant_dynamic-update-slice_fusion.1 = (bf16[16,2304]{1,0:T(8,128)(2,1)S(1)}, bf16[128,2304]{1,0:T(8,128)(2,1)S(1)}) fusion(bf16[16,1152]{1,0:T(8,128)(2,1)} %param.7), kind=kLoop, calls=%fused_computation.3 | loop fusion | bytes 110592
  0.8 0.0 copy-start
  0.8 0.9 %constant_dynamic-update-slice_fusion = (bf16[16,2304]{1,0:T(8,128)(2,1)S(1)}, bf16[128,2304]{1,0:T(8,128)(2,1)S(1)}) fusion(bf16[16,2304]{1,0:T(8,128)(2,1)S(1)} %get-tuple-element.7, bf16[16,1152]{1,0:T(8,128)(2,1)} %param.8, bf16[128,2304]{1,0:T(8,128)(2,1)S(1)} %get-tuple-element.8), kind=kLoop, calls=%fused_computation.2 | loop fusion | bytes 110592 | tf_op jit(solution)/shard_map/concatenate | solution.py:104
  1.7 5.1 %collective-permute-start.2 = (bf16[16,2304]{1,0:T(8,128)(2,1)S(1)}, bf16[16,2304]{1,0:T(8,128)(2,1)S(1)}, u32[]{:S(2)}, u32[]{:S(2)}) collective-permute-start(bf16[16,2304]{1,0:T(8,128)(2,1)S(1)} %get-tuple-element.5), channel_id=1, source_target_pairs={{0,12},{2,14},{4,8},{6,10},{8,4},{10,6},{12,0},{14,2},{1,13},{3,15... | collective-permute-start | bytes 221192 | tf_op jit(solution)/shard_map/ppermute | solution.py:15
  6.8 0.0 collective-permute-start.1
  6.8 0.6 %collective-permute-start = (bf16[16,2304]{1,0:T(8,128)(2,1)S(1)}, bf16[16,2304]{1,0:T(8,128)(2,1)S(1)}, u32[]{:S(2)}, u32[]{:S(2)}) collective-permute-start(bf16[16,2304]{1,0:T(8,128)(2,1)S(1)} %get-tuple-element.5), channel_id=1, source_target_pairs={{0,4},{2,6},{4,0},{6,2},{8,12},{10,14},{12,8},{14,10},{1,5},{3,7},... | collective-permute-start | bytes 221192 | tf_op jit(solution)/shard_map/ppermute | solution.py:15
  7.4 1.6 %collective-permute-start.3 = (bf16[16,2304]{1,0:T(8,128)(2,1)S(1)}, bf16[16,2304]{1,0:T(8,128)(2,1)S(1)}, u32[]{:S(2)}, u32[]{:S(2)}) collective-permute-start(bf16[16,2304]{1,0:T(8,128)(2,1)S(1)} %get-tuple-element.5), channel_id=1, source_target_pairs={{0,2},{2,0},{4,6},{6,4},{8,10},{10,8},{12,14},{14,12},{1,3},{3,1},... | collective-permute-start | bytes 221192 | tf_op jit(solution)/shard_map/ppermute | solution.py:15
  9.1 0.0 collective-permute-start.8
  9.1 0.4 %collective-permute-done.2 = bf16[16,2304]{1,0:T(8,128)(2,1)S(1)} collective-permute-done((bf16[16,2304]{1,0:T(8,128)(2,1)S(1)}, bf16[16,2304]{1,0:T(8,128)(2,1)S(1)}, u32[]{:S(2)}, u32[]{:S(2)}) %collective-permute-start.2) | collective-permute-done | bytes 73760 | tf_op jit(solution)/shard_map/ppermute | solution.py:15
  9.4 1.9 %collective-permute-start.6 = (bf16[16,2304]{1,0:T(8,128)(2,1)S(1)}, bf16[16,2304]{1,0:T(8,128)(2,1)S(1)}, u32[]{:S(2)}, u32[]{:S(2)}) collective-permute-start(bf16[16,2304]{1,0:T(8,128)(2,1)S(1)} %collective-permute-done.2), channel_id=1, source_target_pairs={{0,2},{2,0},{4,6},{6,4},{8,10},{10,8},{12,14},{14,12},{1,3},{3,1},... | collective-permute-start | bytes 221192 | tf_op jit(solution)/shard_map/ppermute | solution.py:15
  11.3 1.7 %collective-permute-done.1 = bf16[16,2304]{1,0:T(8,128)(2,1)S(1)} collective-permute-done((bf16[16,2304]{1,0:T(8,128)(2,1)S(1)}, bf16[16,2304]{1,0:T(8,128)(2,1)S(1)}, u32[]{:S(2)}, u32[]{:S(2)}) %collective-permute-start.1) | collective-permute-done | bytes 73760 | tf_op jit(solution)/shard_map/ppermute | solution.py:15
  13.0 1.5 %collective-permute-start.5 = (bf16[16,2304]{1,0:T(8,128)(2,1)S(1)}, bf16[16,2304]{1,0:T(8,128)(2,1)S(1)}, u32[]{:S(2)}, u32[]{:S(2)}) collective-permute-start(bf16[16,2304]{1,0:T(8,128)(2,1)S(1)} %collective-permute-done.1), channel_id=1, source_target_pairs={{0,2},{2,0},{4,6},{6,4},{8,10},{10,8},{12,14},{14,12},{1,3},{3,1},... | collective-permute-start | bytes 221192 | tf_op jit(solution)/shard_map/ppermute | solution.py:15
  14.5 0.0 collective-permute-done
  14.5 0.5 %collective-permute-start.4 = (bf16[16,2304]{1,0:T(8,128)(2,1)S(1)}, bf16[16,2304]{1,0:T(8,128)(2,1)S(1)}, u32[]{:S(2)}, u32[]{:S(2)}) collective-permute-start(bf16[16,2304]{1,0:T(8,128)(2,1)S(1)} %collective-permute-done), channel_id=1, source_target_pairs={{0,2},{2,0},{4,6},{6,4},{8,10},{10,8},{12,14},{14,12},{1,3},{3,1},... | collective-permute-start | bytes 221192 | tf_op jit(solution)/shard_map/ppermute | solution.py:15
  15.1 0.0 collective-permute-done.3
  15.1 3.8 %collective-permute-done.4 = bf16[16,2304]{1,0:T(8,128)(2,1)S(1)} collective-permute-done((bf16[16,2304]{1,0:T(8,128)(2,1)S(1)}, bf16[16,2304]{1,0:T(8,128)(2,1)S(1)}, u32[]{:S(2)}, u32[]{:S(2)}) %collective-permute-start.4) | collective-permute-done | bytes 73760 | tf_op jit(solution)/shard_map/ppermute | solution.py:15
  18.9 0.0 collective-permute-done.5
  18.9 0.0 collective-permute-done.6
  18.9 0.0 copy-start.1
  18.9 0.1 collective-permute-start.7
  19.0 0.7 %tile.4 = f32[12,96]{1,0:T(8,128)S(1)} broadcast(f32[96]{0:T(128)} %param.9), dimensions={1} | broadcast | bytes 4992 | tf_op jit(solution)/shard_map/tile | solution.py:109
  19.7 0.1 stack_tile.6
  19.8 0.7 %tile.5 = f32[12,96]{1,0:T(8,128)S(1)} broadcast(f32[96]{0:T(128)} %param.10), dimensions={1} | broadcast | bytes 4992 | tf_op jit(solution)/shard_map/tile | solution.py:109
  20.4 0.1 stack_tile.7
  20.5 0.6 %pad_maximum_fusion.gain_ref = f32[2,1152]{1,0:T(2,128)} fusion(f32[1,1152]{1,0:T(1,128)S(1)} %stack_tile.7, f32[1,1152]{1,0:T(1,128)S(1)} %stack_tile.6), kind=kLoop, calls=%fused_computation.22 | loop fusion | flops 2304 | bytes 18432 | tf_op jit(solution)/shard_map/stack | solution.py:109
  21.1 0.0 collective-permute-done.7.theirs_ref
  21.1 0.0 copy-done.1
  21.1 4.1 %shard_map.64 = bf16[16,1152]{1,0:T(8,128)(2,1)} custom-call(bf16[16,1152]{1,0:T(8,128)(2,1)} %q_ref.1, bf16[128,2304]{1,0:T(8,128)(2,1)} %copy-done.1, bf16[128,2304]{1,0:T(8,128)(2,1)} %collective-permute-done.7.theirs_ref, f32[2,1152]{1,0:T(2,128)} %pad_maximum_fusion.gain_ref), custom_call_target="tpu_custom_call" | custom-call | tf_op jit(solution)/shard_map/pallas_call | solution.py:110
  25.2 0.0 copy-start.2
  25.2 0.0 collective-permute-done.8
  25.2 2.3 %fusion.1 = f32[16,2304]{1,0:T(8,128)S(1)} fusion(bf16[576,2304]{1,0:T(8,128)(2,1)} %collective-permute-done.8, pred[]{:T(512)S(6)} %eq.3, bf16[16,1152]{1,0:T(8,128)(2,1)} %shard_map.64), kind=kOutput, calls=%fused_computation.13 | convolution fusion | flops 42476544 | bytes 2842625 | tf_op jit(solution)/shard_map/dot_general | solution.py:40
  27.5 0.0 copy-done
  27.5 0.0 copy-done.2
  27.5 1.1 %fusion = bf16[16,2304]{1,0:T(8,128)(2,1)} fusion(f32[16,2304]{1,0:T(8,128)S(1)} %fusion.1, bf16[576,2304]{1,0:T(8,128)(2,1)S(1)} %copy-done, pred[]{:T(512)S(6)} %eq.3, bf16[16,1152]{1,0:T(8,128)(2,1)S(1)} %copy-done.2), kind=kOutput, calls=%fused_computation.1 | convolution fusion | flops 42550272 | bytes 2916353 | tf_op jit(solution)/shard_map/dot_general | solution.py:40
  (7 shorter events, 0.0 us)
Async XLA Ops:
  0.8 26.8 %copy-start = (bf16[576,2304]{1,0:T(8,128)(2,1)S(1)}, bf16[576,2304]{1,0:T(8,128)(2,1)}, u32[]{:S(2)}) copy-start(bf16[576,2304]{1,0:T(8,128)(2,1)} %param.11) | copy-start | bytes 7962628
  1.7 7.7 %collective-permute-start.2 = (bf16[16,2304]{1,0:T(8,128)(2,1)S(1)}, bf16[16,2304]{1,0:T(8,128)(2,1)S(1)}, u32[]{:S(2)}, u32[]{:S(2)}) collective-permute-start(bf16[16,2304]{1,0:T(8,128)(2,1)S(1)} %get-tuple-element.5), channel_id=1, source_target_pairs={{0,12},{2,14},{4,8},{6,10},{8,4},{10,6},{12,0},{14,2},{1,13},{3,15... | collective-permute-start | bytes 221192 | tf_op jit(solution)/shard_map/ppermute | solution.py:15
  6.8 6.2 %collective-permute-start.1 = (bf16[16,2304]{1,0:T(8,128)(2,1)S(1)}, bf16[16,2304]{1,0:T(8,128)(2,1)S(1)}, u32[]{:S(2)}, u32[]{:S(2)}) collective-permute-start(bf16[16,2304]{1,0:T(8,128)(2,1)S(1)} %get-tuple-element.5), channel_id=1, source_target_pairs={{0,8},{2,10},{4,12},{6,14},{8,0},{10,2},{12,4},{14,6},{1,9},{3,11}... | collective-permute-start | bytes 221192 | tf_op jit(solution)/shard_map/ppermute | solution.py:15
  6.8 7.7 %collective-permute-start = (bf16[16,2304]{1,0:T(8,128)(2,1)S(1)}, bf16[16,2304]{1,0:T(8,128)(2,1)S(1)}, u32[]{:S(2)}, u32[]{:S(2)}) collective-permute-start(bf16[16,2304]{1,0:T(8,128)(2,1)S(1)} %get-tuple-element.5), channel_id=1, source_target_pairs={{0,4},{2,6},{4,0},{6,2},{8,12},{10,14},{12,8},{14,10},{1,5},{3,7},... | collective-permute-start | bytes 221192 | tf_op jit(solution)/shard_map/ppermute | solution.py:15
  7.4 7.6 %collective-permute-start.3 = (bf16[16,2304]{1,0:T(8,128)(2,1)S(1)}, bf16[16,2304]{1,0:T(8,128)(2,1)S(1)}, u32[]{:S(2)}, u32[]{:S(2)}) collective-permute-start(bf16[16,2304]{1,0:T(8,128)(2,1)S(1)} %get-tuple-element.5), channel_id=1, source_target_pairs={{0,2},{2,0},{4,6},{6,4},{8,10},{10,8},{12,14},{14,12},{1,3},{3,1},... | collective-permute-start | bytes 221192 | tf_op jit(solution)/shard_map/ppermute | solution.py:15
  9.1 16.2 %collective-permute-start.8 = (bf16[576,2304]{1,0:T(8,128)(2,1)}, bf16[576,2304]{1,0:T(8,128)(2,1)}, u32[]{:S(2)}, u32[]{:S(2)}) collective-permute-start(bf16[576,2304]{1,0:T(8,128)(2,1)} %param.11), channel_id=1, source_target_pairs={{0,1},{1,0},{2,3},{3,2},{4,5},{5,4},{6,7},{7,6},{8,9},{9,8},{10,11... | collective-permute-start | bytes 7962632 | tf_op jit(solution)/shard_map/ppermute | solution.py:15
  9.4 9.4 %collective-permute-start.6 = (bf16[16,2304]{1,0:T(8,128)(2,1)S(1)}, bf16[16,2304]{1,0:T(8,128)(2,1)S(1)}, u32[]{:S(2)}, u32[]{:S(2)}) collective-permute-start(bf16[16,2304]{1,0:T(8,128)(2,1)S(1)} %collective-permute-done.2), channel_id=1, source_target_pairs={{0,2},{2,0},{4,6},{6,4},{8,10},{10,8},{12,14},{14,12},{1,3},{3,1},... | collective-permute-start | bytes 221192 | tf_op jit(solution)/shard_map/ppermute | solution.py:15
  13.0 5.9 %collective-permute-start.5 = (bf16[16,2304]{1,0:T(8,128)(2,1)S(1)}, bf16[16,2304]{1,0:T(8,128)(2,1)S(1)}, u32[]{:S(2)}, u32[]{:S(2)}) collective-permute-start(bf16[16,2304]{1,0:T(8,128)(2,1)S(1)} %collective-permute-done.1), channel_id=1, source_target_pairs={{0,2},{2,0},{4,6},{6,4},{8,10},{10,8},{12,14},{14,12},{1,3},{3,1},... | collective-permute-start | bytes 221192 | tf_op jit(solution)/shard_map/ppermute | solution.py:15
  14.5 4.4 %collective-permute-start.4 = (bf16[16,2304]{1,0:T(8,128)(2,1)S(1)}, bf16[16,2304]{1,0:T(8,128)(2,1)S(1)}, u32[]{:S(2)}, u32[]{:S(2)}) collective-permute-start(bf16[16,2304]{1,0:T(8,128)(2,1)S(1)} %collective-permute-done), channel_id=1, source_target_pairs={{0,2},{2,0},{4,6},{6,4},{8,10},{10,8},{12,14},{14,12},{1,3},{3,1},... | collective-permute-start | bytes 221192 | tf_op jit(solution)/shard_map/ppermute | solution.py:15
  18.9 2.2 %copy-start.1 = (bf16[128,2304]{1,0:T(8,128)(2,1)}, bf16[128,2304]{1,0:T(8,128)(2,1)S(1)}, u32[]{:S(2)}) copy-start(bf16[128,2304]{1,0:T(8,128)(2,1)S(1)} %constant_dynamic-update-slice_fusion.2.mine_ref) | copy-start | bytes 1769476
  18.9 2.2 %collective-permute-start.7 = (bf16[128,2304]{1,0:T(8,128)(2,1)S(1)}, bf16[128,2304]{1,0:T(8,128)(2,1)}, u32[]{:S(2)}, u32[]{:S(2)}) collective-permute-start(bf16[128,2304]{1,0:T(8,128)(2,1)S(1)} %constant_dynamic-update-slice_fusion.2.mine_ref), channel_id=1, source_target_pairs={{0,1},{1,0},{2,3},{3,2},{4,5},{5,4},{6,7},{7,6},{8,9},{9,8},{10,11... | collective-permute-start | bytes 1769480 | tf_op jit(solution)/shard_map/ppermute | solution.py:15
  25.2 2.3 %copy-start.2 = (bf16[16,1152]{1,0:T(8,128)(2,1)S(1)}, bf16[16,1152]{1,0:T(8,128)(2,1)}, u32[]{:S(2)}) copy-start(bf16[16,1152]{1,0:T(8,128)(2,1)} %shard_map.64) | copy-start | bytes 110596

commit v2 on v1

--- a/solution.py
+++ b/solution.py
@@ -48,30 +48,66 @@
     return (grid * wide * gain).astype(jnp.bfloat16)
 
 
-def attend_kernel(q_ref, mine_ref, theirs_ref, gain_ref, out_ref):
-    rows, width = q_ref.shape
+def widened(gain):
+    channel = lax.broadcasted_iota(jnp.int32, (HD, H * HD), 0)
+    lane = lax.broadcasted_iota(jnp.int32, (HD, H * HD), 1)
+    hit = lane == channel
+    for h in range(1, H):
+        hit = hit | (lane == channel + h * HD)
+    spread = hit.astype(jnp.bfloat16)
+    return sum(dot(part, spread) for part in pieces(gain, 3))
+
+
+def partial_attention(stacked, held_ref, key_gain, masks, rows):
+    width = key_gain.shape[1]
     gather = lane_of(width, 128).astype(jnp.bfloat16)
     spread = head_of(128, width).astype(jnp.bfloat16)
-    key = jnp.concatenate([mine_ref[:, :width], theirs_ref[:, :width]], 0)
-    value = jnp.concatenate([mine_ref[:, width:], theirs_ref[:, width:]], 0)
-    query_n = normed_rows(q_ref[...], gain_ref[0:1, :], gather, spread)
-    key_n = normed_rows(key, gain_ref[1:2, :], gather, spread)
-    lane = lax.broadcasted_iota(jnp.int32, (rows, width), 1)
-    masks = [(lane >= h * HD) & (lane < (h + 1) * HD) for h in range(H)]
-    query_f = query_n.astype(jnp.float32)
-    stacked = jnp.concatenate([jnp.where(m, query_f, 0.0) for m in masks], 0).astype(jnp.bfloat16)
+    key_n = normed_rows(held_ref[:, :width], key_gain, gather, spread)
     scores = lax.dot_general(
         stacked, key_n, (((1,), (1,)), ((), ())), preferred_element_type=jnp.float32
     ) * (float(HD) ** (-0.5))
     expd = jnp.exp(scores)
     total = jnp.sum(expd, axis=1, keepdims=True)
-    weighted = dot(expd.astype(jnp.bfloat16), value)
+    weighted = dot(expd.astype(jnp.bfloat16), held_ref[:, width:])
     top = jnp.zeros((rows, width), jnp.float32)
     below = jnp.zeros((rows, width), jnp.float32)
     for h in range(H):
         top = jnp.where(masks[h], weighted[h * rows : (h + 1) * rows], top)
         below = jnp.where(masks[h], total[h * rows : (h + 1) * rows], below)
-    out_ref[...] = (top / below).astype(out_ref.dtype)
+    return top, below
+
+
+def masks_of(rows, width):
+    lane = lax.broadcasted_iota(jnp.int32, (rows, width), 1)
+    return [(lane >= h * HD) & (lane < (h + 1) * HD) for h in range(H)]
+
+
+def first_kernel(q_ref, mine_ref, q_gain_ref, k_gain_ref, stacked_ref, gain_ref, top_ref, below_ref):
+    rows, width = q_ref.shape
+    masks = masks_of(rows, width)
+    gather = lane_of(width, 128).astype(jnp.bfloat16)
+    spread = head_of(128, width).astype(jnp.bfloat16)
+    query_f = normed_rows(q_ref[...], widened(q_gain_ref[...]), gather, spread).astype(jnp.float32)
+    stacked = jnp.concatenate([jnp.where(m, query_f, 0.0) for m in masks], 0).astype(jnp.bfloat16)
+    key_gain = widened(k_gain_ref[...])
+    stacked_ref[...] = stacked
+    gain_ref[...] = key_gain
+    top_ref[...], below_ref[...] = partial_attention(stacked, mine_ref, key_gain, masks, rows)
+
+
+def second_kernel(
+    theirs_ref, stacked_ref, gain_ref, top_ref, below_ref, own_w_ref, other_w_ref, out_ref
+):
+    rows, width = top_ref.shape
+    masks = masks_of(rows, width)
+    top, below = partial_attention(stacked_ref[...], theirs_ref, gain_ref[...], masks, rows)
+    attn = (top_ref[...] + top) / (below_ref[...] + below)
+    half = width // 2
+    low, high = attn[:, :half], attn[:, half:]
+    first = lax.axis_index("uly") == 0
+    own = jnp.where(first, low, high).astype(jnp.bfloat16)
+    other = jnp.where(first, high, low).astype(jnp.bfloat16)
+    out_ref[...] = (dot(own, own_w_ref[...]) + dot(other, other_w_ref[...])).astype(out_ref.dtype)
 
 
 def normed(data, gain):
@@ -106,18 +142,30 @@
     held += [swap(block, "blk", 1) for block in held]
     mine = jnp.concatenate(held, 0)
     theirs = swap(mine, "uly", 1)
-    gains = jnp.stack([jnp.tile(q_gain, H), jnp.tile(k_gain, H)])
-    attn = pl.pallas_call(
-        attend_kernel,
-        out_shape=jax.ShapeDtypeStruct((rows, width), jnp.bfloat16),
-        in_specs=[pl.BlockSpec(memory_space=pltpu.VMEM)] * 4,
-        out_specs=pl.BlockSpec(memory_space=pltpu.VMEM),
-    )(query, mine, theirs, gains)
-    half = width // 2
-    first = lax.axis_index("uly") == 0
-    own = jnp.where(first, attn[:, :half], attn[:, half:])
-    other = jnp.where(first, attn[:, half:], attn[:, :half])
-    return (dot(own, out_weight) + dot(other, other_weight)).astype(jnp.bfloat16)
+    f32 = jnp.float32
+    vmem = pl.BlockSpec(memory_space=pltpu.VMEM)
+    cost = pl.CostEstimate(flops=2_000_000_000, bytes_accessed=2 * mine.size, transcendentals=0)
+    stacked, gain, top, below = pl.pallas_call(
+        first_kernel,
+        out_shape=(
+            jax.ShapeDtypeStruct((H * rows, width), jnp.bfloat16),
+            jax.ShapeDtypeStruct((1, width), f32),
+            jax.ShapeDtypeStruct((rows, width), f32),
+            jax.ShapeDtypeStruct((rows, width), f32),
+        ),
+        in_specs=[vmem] * 4,
+        out_specs=(vmem,) * 4,
+        cost_estimate=cost,
+        compiler_params=pltpu.CompilerParams(vmem_limit_bytes=16 << 20),
+    )(query, mine, q_gain.reshape(1, HD), k_gain.reshape(1, HD))
+    return pl.pallas_call(
+        second_kernel,
+        out_shape=jax.ShapeDtypeStruct((rows, out_weight.shape[1]), jnp.bfloat16),
+        in_specs=[vmem] * 7,
+        out_specs=vmem,
+        cost_estimate=cost,
+        compiler_params=pltpu.CompilerParams(vmem_limit_bytes=24 << 20),
+    )(theirs, stacked, gain, top, below, out_weight, other_weight)
 
 
 def solution(mesh):

time: 29 us -> 26.2 us (0.903)
  matrix products: 3.44 us -> 0 us
  Pallas kernels: 4.1 us -> 4.97 us
  other arithmetic: 0.61 us -> 0 us
  local copies, waits for them, and re-layouts: 3.28 us -> 3.68 us
    dot_general x2 -> x0, matrix products: 3.44 us -> none  [dot(): return jnp.dot(a, b, preferred_element_type=jnp.float32)]
    unnamed x13 -> x15, local copies, waits for them, and re-layouts: 0.82 us -> 2.89 us
    another operation x4 -> x0, local copies, waits for them, and re-layouts: 1.52 us -> none  [direct(): gains = jnp.stack([jnp.tile(q_gain, H), jnp.tile(k_gain, H)])]
    pallas_call x1 -> x2, Pallas kernels: 4.1 us -> 4.97 us  [the longest x1 3.01 us: direct(): pl.pallas_call(second_kernel, out_shape=jax.ShapeDtypeStruct((rows, out_w...]
    another operation x1 -> x0, other arithmetic: 0.61 us -> none  [direct(): gains = jnp.stack([jnp.tile(q_gain, H), jnp.tile(k_gain, H)])]
  transfers between devices with their start and end apart: 9 -> 9, of which waited for: 3 -> 3; matrix products, arithmetic and copies ran while one was open for 8% -> 0% of each run, Pallas kernels for 14% -> 8%
where the time goes in v2:
time: 26.2 us; the launch traced here: 25.9 us
  starting transfers between devices  11.3 us (43%)
  waiting for transfers between devices  5.82 us (22%)
  Pallas kernels  4.97 us (19%)
  local copies, waits for them, and re-layouts  3.68 us (14%)
    ppermute x9, starting transfers between devices, swap(): return lax.ppermute(block, axis, [(i, i ^ mask) for i in range(count)])  11.3 us
    ppermute x9, waiting for transfers between devices, swap(): return lax.ppermute(block, axis, [(i, i ^ mask) for i in range(count)])  5.82 us
    pallas_call x1, Pallas kernels, direct(): pl.pallas_call(second_kernel, out_shape=jax.ShapeDtypeStruct((rows, out_w...  3.01 us
    unnamed x15, local copies, waits for them, and re-layouts  2.89 us
    pallas_call x1, Pallas kernels, direct(): pl.pallas_call(first_kernel, out_shape=(jax.ShapeDtypeStruct((H * rows, w...  1.96 us
    concatenate x1, local copies, waits for them, and re-layouts, direct(): held = [jnp.concatenate([key, value], 1)]  0.78 us
  transfers between devices with their start and end apart: 9, of which 3 were waited for; matrix products, arithmetic and copies ran while one was open for 0% of the time, Pallas kernels for 8%

profile of v2, /device:TPU:0, one launch (start us, length us, event | category | flops | bytes accessed | tf_op | source)
XLA Modules:
  0.0 25.9 jit_solution(6269496022384089212)
XLA Ops:
  0.0 0.8 %constant_dynamic-update-slice_fusion.1 = (bf16[16,2304]{1,0:T(8,128)(2,1)S(1)}, bf16[128,2304]{1,0:T(8,128)(2,1)S(1)}) fusion(bf16[16,1152]{1,0:T(8,128)(2,1)} %param.7), kind=kLoop, calls=%fused_computation.1 | loop fusion | bytes 110592
  0.8 0.8 %constant_dynamic-update-slice_fusion = (bf16[16,2304]{1,0:T(8,128)(2,1)S(1)}, bf16[128,2304]{1,0:T(8,128)(2,1)S(1)}) fusion(bf16[16,2304]{1,0:T(8,128)(2,1)S(1)} %get-tuple-element.15, bf16[16,1152]{1,0:T(8,128)(2,1)} %param.8, bf16[128,2304]{1,0:T(8,128)(2,1)S(1)} %get-tuple-element.16), kind=kLoop, calls=%fused_computation | loop fusion | bytes 110592 | tf_op jit(solution)/shard_map/concatenate | solution.py:140
  1.6 5.1 %collective-permute-start.2 = (bf16[16,2304]{1,0:T(8,128)(2,1)S(1)}, bf16[16,2304]{1,0:T(8,128)(2,1)S(1)}, u32[]{:S(2)}, u32[]{:S(2)}) collective-permute-start(bf16[16,2304]{1,0:T(8,128)(2,1)S(1)} %get-tuple-element.13), channel_id=1, source_target_pairs={{0,12},{2,14},{4,8},{6,10},{8,4},{10,6},{12,0},{14,2},{1,13},{3,15... | collective-permute-start | bytes 221192 | tf_op jit(solution)/shard_map/ppermute | solution.py:15
  6.6 0.0 collective-permute-start.1
  6.6 0.6 %collective-permute-start = (bf16[16,2304]{1,0:T(8,128)(2,1)S(1)}, bf16[16,2304]{1,0:T(8,128)(2,1)S(1)}, u32[]{:S(2)}, u32[]{:S(2)}) collective-permute-start(bf16[16,2304]{1,0:T(8,128)(2,1)S(1)} %get-tuple-element.13), channel_id=1, source_target_pairs={{0,4},{2,6},{4,0},{6,2},{8,12},{10,14},{12,8},{14,10},{1,5},{3,7},... | collective-permute-start | bytes 221192 | tf_op jit(solution)/shard_map/ppermute | solution.py:15
  7.3 1.6 %collective-permute-start.3 = (bf16[16,2304]{1,0:T(8,128)(2,1)S(1)}, bf16[16,2304]{1,0:T(8,128)(2,1)S(1)}, u32[]{:S(2)}, u32[]{:S(2)}) collective-permute-start(bf16[16,2304]{1,0:T(8,128)(2,1)S(1)} %get-tuple-element.13), channel_id=1, source_target_pairs={{0,2},{2,0},{4,6},{6,4},{8,10},{10,8},{12,14},{14,12},{1,3},{3,1},... | collective-permute-start | bytes 221192 | tf_op jit(solution)/shard_map/ppermute | solution.py:15
  8.9 0.0 collective-permute-start.8
  8.9 0.4 %collective-permute-done.2 = bf16[16,2304]{1,0:T(8,128)(2,1)S(1)} collective-permute-done((bf16[16,2304]{1,0:T(8,128)(2,1)S(1)}, bf16[16,2304]{1,0:T(8,128)(2,1)S(1)}, u32[]{:S(2)}, u32[]{:S(2)}) %collective-permute-start.2) | collective-permute-done | bytes 73760 | tf_op jit(solution)/shard_map/ppermute | solution.py:15
  9.3 1.9 %collective-permute-start.6 = (bf16[16,2304]{1,0:T(8,128)(2,1)S(1)}, bf16[16,2304]{1,0:T(8,128)(2,1)S(1)}, u32[]{:S(2)}, u32[]{:S(2)}) collective-permute-start(bf16[16,2304]{1,0:T(8,128)(2,1)S(1)} %collective-permute-done.2), channel_id=1, source_target_pairs={{0,2},{2,0},{4,6},{6,4},{8,10},{10,8},{12,14},{14,12},{1,3},{3,1},... | collective-permute-start | bytes 221192 | tf_op jit(solution)/shard_map/ppermute | solution.py:15
  11.2 1.7 %collective-permute-done.1 = bf16[16,2304]{1,0:T(8,128)(2,1)S(1)} collective-permute-done((bf16[16,2304]{1,0:T(8,128)(2,1)S(1)}, bf16[16,2304]{1,0:T(8,128)(2,1)S(1)}, u32[]{:S(2)}, u32[]{:S(2)}) %collective-permute-start.1) | collective-permute-done | bytes 73760 | tf_op jit(solution)/shard_map/ppermute | solution.py:15
  12.8 1.5 %collective-permute-start.5 = (bf16[16,2304]{1,0:T(8,128)(2,1)S(1)}, bf16[16,2304]{1,0:T(8,128)(2,1)S(1)}, u32[]{:S(2)}, u32[]{:S(2)}) collective-permute-start(bf16[16,2304]{1,0:T(8,128)(2,1)S(1)} %collective-permute-done.1), channel_id=1, source_target_pairs={{0,2},{2,0},{4,6},{6,4},{8,10},{10,8},{12,14},{14,12},{1,3},{3,1},... | collective-permute-start | bytes 221192 | tf_op jit(solution)/shard_map/ppermute | solution.py:15
  14.3 0.0 collective-permute-done
  14.3 0.5 %collective-permute-start.4 = (bf16[16,2304]{1,0:T(8,128)(2,1)S(1)}, bf16[16,2304]{1,0:T(8,128)(2,1)S(1)}, u32[]{:S(2)}, u32[]{:S(2)}) collective-permute-start(bf16[16,2304]{1,0:T(8,128)(2,1)S(1)} %collective-permute-done), channel_id=1, source_target_pairs={{0,2},{2,0},{4,6},{6,4},{8,10},{10,8},{12,14},{14,12},{1,3},{3,1},... | collective-permute-start | bytes 221192 | tf_op jit(solution)/shard_map/ppermute | solution.py:15
  14.9 0.0 collective-permute-done.3
  14.9 3.8 %collective-permute-done.4 = bf16[16,2304]{1,0:T(8,128)(2,1)S(1)} collective-permute-done((bf16[16,2304]{1,0:T(8,128)(2,1)S(1)}, bf16[16,2304]{1,0:T(8,128)(2,1)S(1)}, u32[]{:S(2)}, u32[]{:S(2)}) %collective-permute-start.4) | collective-permute-done | bytes 73760 | tf_op jit(solution)/shard_map/ppermute | solution.py:15
  18.7 0.0 collective-permute-done.5
  18.7 0.0 collective-permute-done.6
  18.7 0.1 collective-permute-start.7
  18.8 0.0 copy-start.1
  18.8 0.8 %copy-done.1 = bf16[16,1152]{1,0:T(8,128)(2,1)S(1)} copy-done((bf16[16,1152]{1,0:T(8,128)(2,1)S(1)}, bf16[16,1152]{1,0:T(8,128)(2,1)}, u32[]{:S(2)}) %copy-start.1) | copy-done | bytes 36888
  19.6 0.0 copy-start.2
  19.6 0.7 %copy-done.2 = f32[96]{0:T(128)S(1)} copy-done((f32[96]{0:T(128)S(1)}, f32[96]{0:T(128)}, u32[]{:S(2)}) %copy-start.2) | copy-done | bytes 408
  20.3 0.0 copy-start.3
  20.3 0.7 %copy-done.3 = f32[96]{0:T(128)S(1)} copy-done((f32[96]{0:T(128)S(1)}, f32[96]{0:T(128)}, u32[]{:S(2)}) %copy-start.3) | copy-done | bytes 408
  20.9 0.0 copy-start
  20.9 2.0 %shard_map.64 = (bf16[192,1152]{1,0:T(8,128)(2,1)S(1)}, f32[1,1152]{1,0:T(1,128)S(1)}, f32[16,1152]{1,0:T(8,128)S(1)}, f32[16,1152]{1,0:T(8,128)S(1)}) custom-call(bf16[16,1152]{1,0:T(8,128)(2,1)S(1)} %copy-done.1, bf16[128,2304]{1,0:T(8,128)(2,1)S(1)} %constant_dynamic-update-slice_fusion.2.mine_ref, f32[1,96]{1,0:T(1,128)S(1)} %bitcast.2, f32[1,96]{1,0:T(1,128)S(1)} %bitcast.3), custom_call_target="tpu_custom_call" | custom-call | flops 2000000000 | bytes 589824 | tf_op jit(solution)/shard_map/pallas_call | solution.py:148
  22.9 0.0 collective-permute-done.7.theirs_ref
  22.9 0.0 collective-permute-done.8.other_w_ref
  22.9 0.0 copy-done
  22.9 3.0 %shard_map.65 = bf16[16,2304]{1,0:T(8,128)(2,1)} custom-call(bf16[128,2304]{1,0:T(8,128)(2,1)S(1)} %collective-permute-done.7.theirs_ref, bf16[192,1152]{1,0:T(8,128)(2,1)S(1)} %get-tuple-element.9.stacked_ref, f32[1,1152]{1,0:T(1,128)S(1)} %get-tuple-element.10.gain_ref, f32[16,1152]{1,0:T(8,128)S(1)} %get-tuple-element.11.top_ref, ...), custom_call_target="tpu_custom_call" | custom-call | flops 2000000000 | bytes 589824 | tf_op jit(solution)/shard_map/pallas_call | solution.py:161
  (7 shorter events, 0.0 us)
Async XLA Ops:
  1.6 7.7 %collective-permute-start.2 = (bf16[16,2304]{1,0:T(8,128)(2,1)S(1)}, bf16[16,2304]{1,0:T(8,128)(2,1)S(1)}, u32[]{:S(2)}, u32[]{:S(2)}) collective-permute-start(bf16[16,2304]{1,0:T(8,128)(2,1)S(1)} %get-tuple-element.13), channel_id=1, source_target_pairs={{0,12},{2,14},{4,8},{6,10},{8,4},{10,6},{12,0},{14,2},{1,13},{3,15... | collective-permute-start | bytes 221192 | tf_op jit(solution)/shard_map/ppermute | solution.py:15
  6.6 6.2 %collective-permute-start.1 = (bf16[16,2304]{1,0:T(8,128)(2,1)S(1)}, bf16[16,2304]{1,0:T(8,128)(2,1)S(1)}, u32[]{:S(2)}, u32[]{:S(2)}) collective-permute-start(bf16[16,2304]{1,0:T(8,128)(2,1)S(1)} %get-tuple-element.13), channel_id=1, source_target_pairs={{0,8},{2,10},{4,12},{6,14},{8,0},{10,2},{12,4},{14,6},{1,9},{3,11}... | collective-permute-start | bytes 221192 | tf_op jit(solution)/shard_map/ppermute | solution.py:15
  6.6 7.7 %collective-permute-start = (bf16[16,2304]{1,0:T(8,128)(2,1)S(1)}, bf16[16,2304]{1,0:T(8,128)(2,1)S(1)}, u32[]{:S(2)}, u32[]{:S(2)}) collective-permute-start(bf16[16,2304]{1,0:T(8,128)(2,1)S(1)} %get-tuple-element.13), channel_id=1, source_target_pairs={{0,4},{2,6},{4,0},{6,2},{8,12},{10,14},{12,8},{14,10},{1,5},{3,7},... | collective-permute-start | bytes 221192 | tf_op jit(solution)/shard_map/ppermute | solution.py:15
  7.3 7.6 %collective-permute-start.3 = (bf16[16,2304]{1,0:T(8,128)(2,1)S(1)}, bf16[16,2304]{1,0:T(8,128)(2,1)S(1)}, u32[]{:S(2)}, u32[]{:S(2)}) collective-permute-start(bf16[16,2304]{1,0:T(8,128)(2,1)S(1)} %get-tuple-element.13), channel_id=1, source_target_pairs={{0,2},{2,0},{4,6},{6,4},{8,10},{10,8},{12,14},{14,12},{1,3},{3,1},... | collective-permute-start | bytes 221192 | tf_op jit(solution)/shard_map/ppermute | solution.py:15
  8.9 14.0 %collective-permute-start.8 = (bf16[576,2304]{1,0:T(8,128)(2,1)}, bf16[576,2304]{1,0:T(8,128)(2,1)S(1)}, u32[]{:S(2)}, u32[]{:S(2)}) collective-permute-start(bf16[576,2304]{1,0:T(8,128)(2,1)} %own_w_ref.1), channel_id=1, source_target_pairs={{0,1},{1,0},{2,3},{3,2},{4,5},{5,4},{6,7},{7,6},{8,9},{9,8},{10,11... | collective-permute-start | bytes 7962632 | tf_op jit(solution)/shard_map/ppermute | solution.py:15
  9.3 9.4 %collective-permute-start.6 = (bf16[16,2304]{1,0:T(8,128)(2,1)S(1)}, bf16[16,2304]{1,0:T(8,128)(2,1)S(1)}, u32[]{:S(2)}, u32[]{:S(2)}) collective-permute-start(bf16[16,2304]{1,0:T(8,128)(2,1)S(1)} %collective-permute-done.2), channel_id=1, source_target_pairs={{0,2},{2,0},{4,6},{6,4},{8,10},{10,8},{12,14},{14,12},{1,3},{3,1},... | collective-permute-start | bytes 221192 | tf_op jit(solution)/shard_map/ppermute | solution.py:15
  12.8 5.9 %collective-permute-start.5 = (bf16[16,2304]{1,0:T(8,128)(2,1)S(1)}, bf16[16,2304]{1,0:T(8,128)(2,1)S(1)}, u32[]{:S(2)}, u32[]{:S(2)}) collective-permute-start(bf16[16,2304]{1,0:T(8,128)(2,1)S(1)} %collective-permute-done.1), channel_id=1, source_target_pairs={{0,2},{2,0},{4,6},{6,4},{8,10},{10,8},{12,14},{14,12},{1,3},{3,1},... | collective-permute-start | bytes 221192 | tf_op jit(solution)/shard_map/ppermute | solution.py:15
  14.3 4.4 %collective-permute-start.4 = (bf16[16,2304]{1,0:T(8,128)(2,1)S(1)}, bf16[16,2304]{1,0:T(8,128)(2,1)S(1)}, u32[]{:S(2)}, u32[]{:S(2)}) collective-permute-start(bf16[16,2304]{1,0:T(8,128)(2,1)S(1)} %collective-permute-done), channel_id=1, source_target_pairs={{0,2},{2,0},{4,6},{6,4},{8,10},{10,8},{12,14},{14,12},{1,3},{3,1},... | collective-permute-start | bytes 221192 | tf_op jit(solution)/shard_map/ppermute | solution.py:15
  18.7 4.1 %collective-permute-start.7 = (bf16[128,2304]{1,0:T(8,128)(2,1)S(1)}, bf16[128,2304]{1,0:T(8,128)(2,1)S(1)}, u32[]{:S(2)}, u32[]{:S(2)}) collective-permute-start(bf16[128,2304]{1,0:T(8,128)(2,1)S(1)} %constant_dynamic-update-slice_fusion.2.mine_ref), channel_id=1, source_target_pairs={{0,1},{1,0},{2,3},{3,2},{4,5},{5,4},{6,7},{7,6},{8,9},{9,8},{10,11... | collective-permute-start | bytes 1769480 | tf_op jit(solution)/shard_map/ppermute | solution.py:15
  18.8 0.8 %copy-start.1 = (bf16[16,1152]{1,0:T(8,128)(2,1)S(1)}, bf16[16,1152]{1,0:T(8,128)(2,1)}, u32[]{:S(2)}) copy-start(bf16[16,1152]{1,0:T(8,128)(2,1)} %q_ref.1) | copy-start | bytes 110596
  19.6 0.7 %copy-start.2 = (f32[96]{0:T(128)S(1)}, f32[96]{0:T(128)}, u32[]{:S(2)}) copy-start(f32[96]{0:T(128)} %param.9) | copy-start | bytes 1156
  20.3 0.7 %copy-start.3 = (f32[96]{0:T(128)S(1)}, f32[96]{0:T(128)}, u32[]{:S(2)}) copy-start(f32[96]{0:T(128)} %param.10) | copy-start | bytes 1156
  20.9 2.0 %copy-start = (bf16[576,2304]{1,0:T(8,128)(2,1)S(1)}, bf16[576,2304]{1,0:T(8,128)(2,1)}, u32[]{:S(2)}) copy-start(bf16[576,2304]{1,0:T(8,128)(2,1)} %own_w_ref.1) | copy-start | bytes 7962628

commit v3 on v2

--- a/solution.py
+++ b/solution.py
@@ -82,17 +82,33 @@
     return [(lane >= h * HD) & (lane < (h + 1) * HD) for h in range(H)]
 
 
-def first_kernel(q_ref, mine_ref, q_gain_ref, k_gain_ref, stacked_ref, gain_ref, top_ref, below_ref):
+def query_kernel(
+    q_any, q_gain_any, k_gain_any, stacked_ref, gain_ref, q_ref, q_gain_ref, k_gain_ref, sems
+):
+    copies = [
+        pltpu.make_async_copy(q_any, q_ref, sems.at[0]),
+        pltpu.make_async_copy(q_gain_any, q_gain_ref, sems.at[1]),
+        pltpu.make_async_copy(k_gain_any, k_gain_ref, sems.at[2]),
+    ]
+    for copy in copies:
+        copy.start()
+    for copy in copies:
+        copy.wait()
     rows, width = q_ref.shape
     masks = masks_of(rows, width)
     gather = lane_of(width, 128).astype(jnp.bfloat16)
     spread = head_of(128, width).astype(jnp.bfloat16)
     query_f = normed_rows(q_ref[...], widened(q_gain_ref[...]), gather, spread).astype(jnp.float32)
-    stacked = jnp.concatenate([jnp.where(m, query_f, 0.0) for m in masks], 0).astype(jnp.bfloat16)
-    key_gain = widened(k_gain_ref[...])
-    stacked_ref[...] = stacked
-    gain_ref[...] = key_gain
-    top_ref[...], below_ref[...] = partial_attention(stacked, mine_ref, key_gain, masks, rows)
+    stacked = jnp.concatenate([jnp.where(m, query_f, 0.0) for m in masks], 0)
+    stacked_ref[...] = stacked.astype(jnp.bfloat16)
+    gain_ref[...] = widened(k_gain_ref[...])
+
+
+def first_kernel(mine_ref, stacked_ref, gain_ref, top_ref, below_ref):
+    rows, width = top_ref.shape
+    top_ref[...], below_ref[...] = partial_attention(
+        stacked_ref[...], mine_ref, gain_ref[...], masks_of(rows, width), rows
+    )
 
 
 def second_kernel(
@@ -136,28 +152,45 @@
 def direct(query, key, value, q_gain, k_gain, out_weight):
     rows, width = query.shape
     blocks = lax.axis_size("blk")
-    other_weight = swap(out_weight, "uly", 1)
-    held = [jnp.concatenate([key, value], 1)]
-    held += [swap(held[0], "blk", mask) for mask in range(2, blocks, 2)]
-    held += [swap(block, "blk", 1) for block in held]
-    mine = jnp.concatenate(held, 0)
-    theirs = swap(mine, "uly", 1)
     f32 = jnp.float32
     vmem = pl.BlockSpec(memory_space=pltpu.VMEM)
-    cost = pl.CostEstimate(flops=2_000_000_000, bytes_accessed=2 * mine.size, transcendentals=0)
-    stacked, gain, top, below = pl.pallas_call(
-        first_kernel,
+    cost = pl.CostEstimate(flops=2_000_000_000, bytes_accessed=2 * key.size, transcendentals=0)
+    limit = pltpu.CompilerParams(vmem_limit_bytes=16 << 20)
+    other_weight = swap(out_weight, "uly", 1)
+    held = {0: lax.optimization_barrier(jnp.concatenate([key, value], 1))}
+    far = blocks // 2
+    for mask in [far] * (far > 1) + [1] + [m for m in range(2, blocks, 2) if m != far]:
+        held[mask] = swap(held[0], "blk", mask)
+    for mask in range(2, blocks, 2):
+        held[mask | 1] = swap(held[far], "blk", 1) if mask == far else swap(held[1], "blk", mask)
+    stacked, gain = pl.pallas_call(
+        query_kernel,
         out_shape=(
             jax.ShapeDtypeStruct((H * rows, width), jnp.bfloat16),
             jax.ShapeDtypeStruct((1, width), f32),
-            jax.ShapeDtypeStruct((rows, width), f32),
-            jax.ShapeDtypeStruct((rows, width), f32),
         ),
-        in_specs=[vmem] * 4,
-        out_specs=(vmem,) * 4,
+        in_specs=[pl.BlockSpec(memory_space=pltpu.HBM)] * 3,
+        out_specs=(vmem,) * 2,
+        scratch_shapes=[
+            pltpu.VMEM((rows, width), query.dtype),
+            pltpu.VMEM((1, HD), f32),
+            pltpu.VMEM((1, HD), f32),
+            pltpu.SemaphoreType.DMA((3,)),
+        ],
         cost_estimate=cost,
-        compiler_params=pltpu.CompilerParams(vmem_limit_bytes=16 << 20),
-    )(query, mine, q_gain.reshape(1, HD), k_gain.reshape(1, HD))
+        compiler_params=limit,
+    )(query, q_gain.reshape(1, HD), k_gain.reshape(1, HD))
+    mine = jnp.concatenate([held[m] for m in range(blocks)], 0)
+    mine, stacked, gain = lax.optimization_barrier((mine, stacked, gain))
+    theirs = swap(mine, "uly", 1)
+    top, below = pl.pallas_call(
+        first_kernel,
+        out_shape=(jax.ShapeDtypeStruct((rows, width), f32),) * 2,
+        in_specs=[vmem] * 3,
+        out_specs=(vmem,) * 2,
+        cost_estimate=cost,
+        compiler_params=limit,
+    )(mine, stacked, gain)
     return pl.pallas_call(
         second_kernel,
         out_shape=jax.ShapeDtypeStruct((rows, out_weight.shape[1]), jnp.bfloat16),

time: 26.2 us -> 24.9 us (0.950)
  waiting for transfers between devices: 5.82 us -> 3.75 us
  local copies, waits for them, and re-layouts: 3.68 us -> 2.13 us
  starting transfers between devices: 11.3 us -> 12.6 us
  other arithmetic: 0 us -> 0.79 us
  Pallas kernels: 4.97 us -> 5.3 us
    ppermute x9, waiting for transfers between devices: 5.82 us -> 3.75 us  [swap(): return lax.ppermute(block, axis, [(i, i ^ mask) for i in range(count)])]
    ppermute x9, starting transfers between devices: 11.3 us -> 12.6 us  [swap(): return lax.ppermute(block, axis, [(i, i ^ mask) for i in range(count)])]
    concatenate x0 -> x1, other arithmetic: none -> 0.79 us  [direct(): held = {0: lax.optimization_barrier(jnp.concatenate([key, value], 1))}]
    concatenate x2 -> x1, local copies, waits for them, and re-layouts: 0.79 us -> 0.01 us  [direct(): mine = jnp.concatenate([held[m] for m in range(blocks)], 0)]
    unnamed x15, local copies, waits for them, and re-layouts: 2.89 us -> 2.12 us
    pallas_call x1 -> x2, Pallas kernels: 1.96 us -> 2.28 us  [the longest x1 1.45 us: direct(): pl.pallas_call(first_kernel, out_shape=(jax.ShapeDtypeStruct((rows, width...]
  transfers between devices with their start and end apart: 9 -> 9, of which waited for: 3 -> 2; matrix products, arithmetic and copies ran while one was open for 0% -> 0% of each run, Pallas kernels for 8% -> 9%
where the time goes in v3:
time: 24.9 us; the launch traced here: 24.7 us
  starting transfers between devices  12.6 us (51%)
  Pallas kernels  5.3 us (21%)
  waiting for transfers between devices  3.75 us (15%)
  local copies, waits for them, and re-layouts  2.13 us (9%)
  other arithmetic  0.79 us (3%)
    ppermute x9, starting transfers between devices, swap(): return lax.ppermute(block, axis, [(i, i ^ mask) for i in range(count)])  12.6 us
    ppermute x9, waiting for transfers between devices, swap(): return lax.ppermute(block, axis, [(i, i ^ mask) for i in range(count)])  3.75 us
    pallas_call x1, Pallas kernels, direct(): pl.pallas_call(second_kernel, out_shape=jax.ShapeDtypeStruct((rows, out_w...  3.02 us
    unnamed x15, local copies, waits for them, and re-layouts  2.12 us
    pallas_call x1, Pallas kernels, direct(): pl.pallas_call(first_kernel, out_shape=(jax.ShapeDtypeStruct((rows, width...  1.45 us
    pallas_call x1, Pallas kernels, direct(): pl.pallas_call(query_kernel, out_shape=(jax.ShapeDtypeStruct((H * rows, w...  0.83 us
    concatenate x1, other arithmetic, direct(): held = {0: lax.optimization_barrier(jnp.concatenate([key, value], 1))}  0.79 us
  transfers between devices with their start and end apart: 9, of which 2 were waited for; matrix products, arithmetic and copies ran while one was open for 0% of the time, Pallas kernels for 9%

profile of v3, /device:TPU:0, one launch (start us, length us, event | category | flops | bytes accessed | tf_op | source)
XLA Modules:
  0.0 24.7 jit_solution(14118802036213580758)
XLA Ops:
  0.0 0.8 %pad_maximum_fusion = bf16[16,2304]{1,0:T(8,128)(2,1)S(1)} fusion(bf16[16,1152]{1,0:T(8,128)(2,1)} %param.8, bf16[16,1152]{1,0:T(8,128)(2,1)} %param.7), kind=kLoop, calls=%fused_computation | loop fusion | flops 147456 | bytes 147456 | tf_op jit(solution)/shard_map/concatenate | solution.py:160
  0.8 5.1 %collective-permute-start.5 = (bf16[16,2304]{1,0:T(8,128)(2,1)S(1)}, bf16[16,2304]{1,0:T(8,128)(2,1)S(1)}, u32[]{:S(2)}, u32[]{:S(2)}) collective-permute-start(bf16[16,2304]{1,0:T(8,128)(2,1)S(1)} %pad_maximum_fusion), channel_id=1, source_target_pairs={{0,12},{2,14},{4,8},{6,10},{8,4},{10,6},{12,0},{14,2},{1,13},{3,15... | collective-permute-start | bytes 221192 | tf_op jit(solution)/shard_map/ppermute | solution.py:15
  5.9 0.0 collective-permute-start.3
  5.9 0.6 %collective-permute-start.1 = (bf16[16,2304]{1,0:T(8,128)(2,1)S(1)}, bf16[16,2304]{1,0:T(8,128)(2,1)S(1)}, u32[]{:S(2)}, u32[]{:S(2)}) collective-permute-start(bf16[16,2304]{1,0:T(8,128)(2,1)S(1)} %pad_maximum_fusion), channel_id=1, source_target_pairs={{0,4},{2,6},{4,0},{6,2},{8,12},{10,14},{12,8},{14,10},{1,5},{3,7},... | collective-permute-start | bytes 221192 | tf_op jit(solution)/shard_map/ppermute | solution.py:15
  6.5 1.6 %collective-permute-start = (bf16[16,2304]{1,0:T(8,128)(2,1)S(1)}, bf16[16,2304]{1,0:T(8,128)(2,1)S(1)}, u32[]{:S(2)}, u32[]{:S(2)}) collective-permute-start(bf16[16,2304]{1,0:T(8,128)(2,1)S(1)} %pad_maximum_fusion), channel_id=1, source_target_pairs={{0,2},{2,0},{4,6},{6,4},{8,10},{10,8},{12,14},{14,12},{1,3},{3,1},... | collective-permute-start | bytes 221192 | tf_op jit(solution)/shard_map/ppermute | solution.py:15
  8.2 0.0 collective-permute-start.8
  8.2 0.0 copy-start.1
  8.2 0.8 %copy-done.1 = bf16[16,1152]{1,0:T(8,128)(2,1)S(1)} copy-done((bf16[16,1152]{1,0:T(8,128)(2,1)S(1)}, bf16[16,1152]{1,0:T(8,128)(2,1)}, u32[]{:S(2)}) %copy-start.1) | copy-done | bytes 36888
  8.9 0.0 copy-start.2
  8.9 0.7 %copy-done.2 = f32[96]{0:T(128)S(1)} copy-done((f32[96]{0:T(128)S(1)}, f32[96]{0:T(128)}, u32[]{:S(2)}) %copy-start.2) | copy-done | bytes 408
  9.6 0.0 copy-start.3
  9.6 0.7 %copy-done.3 = f32[96]{0:T(128)S(1)} copy-done((f32[96]{0:T(128)S(1)}, f32[96]{0:T(128)}, u32[]{:S(2)}) %copy-start.3) | copy-done | bytes 408
  10.2 0.8 %shard_map.64 = (bf16[192,1152]{1,0:T(8,128)(2,1)S(1)}, f32[1,1152]{1,0:T(1,128)S(1)}) custom-call(bf16[16,1152]{1,0:T(8,128)(2,1)S(1)} %copy-done.1, f32[1,96]{1,0:T(1,128)S(1)} %bitcast.2, f32[1,96]{1,0:T(1,128)S(1)} %bitcast.3), custom_call_target="tpu_custom_call" | custom-call | flops 2000000000 | bytes 36864 | tf_op jit(solution)/shard_map/pallas_call | solution.py:166
  11.1 0.0 collective-permute-done
  11.1 3.7 %collective-permute-start.6 = (bf16[16,2304]{1,0:T(8,128)(2,1)S(1)}, bf16[16,2304]{1,0:T(8,128)(2,1)S(1)}, u32[]{:S(2)}, u32[]{:S(2)}) collective-permute-start(bf16[16,2304]{1,0:T(8,128)(2,1)S(1)} %collective-permute-done), channel_id=1, source_target_pairs={{0,12},{2,14},{4,8},{6,10},{8,4},{10,6},{12,0},{14,2},{1,13},{3,15... | collective-permute-start | bytes 221192 | tf_op jit(solution)/shard_map/ppermute | solution.py:15
  14.8 0.0 collective-permute-done.3
  14.8 0.1 collective-permute-start.2
  14.9 0.0 collective-permute-done.1
  14.9 1.4 %collective-permute-start.4 = (bf16[16,2304]{1,0:T(8,128)(2,1)S(1)}, bf16[16,2304]{1,0:T(8,128)(2,1)S(1)}, u32[]{:S(2)}, u32[]{:S(2)}) collective-permute-start(bf16[16,2304]{1,0:T(8,128)(2,1)S(1)} %collective-permute-done.3), channel_id=1, source_target_pairs={{0,2},{2,0},{4,6},{6,4},{8,10},{10,8},{12,14},{14,12},{1,3},{3,1},... | collective-permute-start | bytes 221192 | tf_op jit(solution)/shard_map/ppermute | solution.py:15
  16.3 3.2 %collective-permute-done.2 = bf16[16,2304]{1,0:T(8,128)(2,1)S(1)} collective-permute-done((bf16[16,2304]{1,0:T(8,128)(2,1)S(1)}, bf16[16,2304]{1,0:T(8,128)(2,1)S(1)}, u32[]{:S(2)}, u32[]{:S(2)}) %collective-permute-start.2) | collective-permute-done | bytes 73760 | tf_op jit(solution)/shard_map/ppermute | solution.py:15
  19.5 0.0 collective-permute-done.4
  19.5 0.0 collective-permute-done.5
  19.6 0.0 collective-permute-done.6
  19.6 0.0 copy-start
  19.6 0.1 collective-permute-start.7
  19.7 1.4 %shard_map.65 = (f32[16,1152]{1,0:T(8,128)S(1)}, f32[16,1152]{1,0:T(8,128)S(1)}) custom-call(bf16[128,2304]{1,0:T(8,128)(2,1)S(1)} %constant_dynamic-update-slice_fusion.mine_ref, bf16[192,1152]{1,0:T(8,128)(2,1)S(1)} %get-tuple-element.15.stacked_ref, f32[1,1152]{1,0:T(1,128)S(1)} %get-tuple-element.16.gain_ref), custom_call_target="tpu_custom_call" | custom-call | flops 2000000000 | bytes 36864 | tf_op jit(solution)/shard_map/pallas_call | solution.py:186
  21.1 0.5 %collective-permute-done.7.theirs_ref = bf16[128,2304]{1,0:T(8,128)(2,1)S(1)} collective-permute-done((bf16[128,2304]{1,0:T(8,128)(2,1)S(1)}, bf16[128,2304]{1,0:T(8,128)(2,1)S(1)}, u32[]{:S(2)}, u32[]{:S(2)}) %collective-permute-start.7) | collective-permute-done | bytes 589856 | tf_op jit(solution)/shard_map/ppermute | solution.py:15
  21.7 0.0 collective-permute-done.8.other_w_ref
  21.7 0.0 copy-done
  21.7 3.0 %shard_map.66 = bf16[16,2304]{1,0:T(8,128)(2,1)} custom-call(bf16[128,2304]{1,0:T(8,128)(2,1)S(1)} %collective-permute-done.7.theirs_ref, bf16[192,1152]{1,0:T(8,128)(2,1)S(1)} %get-tuple-element.15.stacked_ref, f32[1,1152]{1,0:T(1,128)S(1)} %get-tuple-element.16.gain_ref, f32[16,1152]{1,0:T(8,128)S(1)} %get-tuple-element.17.top_ref, ...), custom_call_target="tpu_custom_call" | custom-call | flops 2000000000 | bytes 36864 | tf_op jit(solution)/shard_map/pallas_call | solution.py:194
  (8 shorter events, 0.1 us)
Async XLA Ops:
  0.8 18.7 %collective-permute-start.5 = (bf16[16,2304]{1,0:T(8,128)(2,1)S(1)}, bf16[16,2304]{1,0:T(8,128)(2,1)S(1)}, u32[]{:S(2)}, u32[]{:S(2)}) collective-permute-start(bf16[16,2304]{1,0:T(8,128)(2,1)S(1)} %pad_maximum_fusion), channel_id=1, source_target_pairs={{0,12},{2,14},{4,8},{6,10},{8,4},{10,6},{12,0},{14,2},{1,13},{3,15... | collective-permute-start | bytes 221192 | tf_op jit(solution)/shard_map/ppermute | solution.py:15
  5.9 8.9 %collective-permute-start.3 = (bf16[16,2304]{1,0:T(8,128)(2,1)S(1)}, bf16[16,2304]{1,0:T(8,128)(2,1)S(1)}, u32[]{:S(2)}, u32[]{:S(2)}) collective-permute-start(bf16[16,2304]{1,0:T(8,128)(2,1)S(1)} %pad_maximum_fusion), channel_id=1, source_target_pairs={{0,8},{2,10},{4,12},{6,14},{8,0},{10,2},{12,4},{14,6},{1,9},{3,11}... | collective-permute-start | bytes 221192 | tf_op jit(solution)/shard_map/ppermute | solution.py:15
  5.9 9.0 %collective-permute-start.1 = (bf16[16,2304]{1,0:T(8,128)(2,1)S(1)}, bf16[16,2304]{1,0:T(8,128)(2,1)S(1)}, u32[]{:S(2)}, u32[]{:S(2)}) collective-permute-start(bf16[16,2304]{1,0:T(8,128)(2,1)S(1)} %pad_maximum_fusion), channel_id=1, source_target_pairs={{0,4},{2,6},{4,0},{6,2},{8,12},{10,14},{12,8},{14,10},{1,5},{3,7},... | collective-permute-start | bytes 221192 | tf_op jit(solution)/shard_map/ppermute | solution.py:15
  6.5 4.6 %collective-permute-start = (bf16[16,2304]{1,0:T(8,128)(2,1)S(1)}, bf16[16,2304]{1,0:T(8,128)(2,1)S(1)}, u32[]{:S(2)}, u32[]{:S(2)}) collective-permute-start(bf16[16,2304]{1,0:T(8,128)(2,1)S(1)} %pad_maximum_fusion), channel_id=1, source_target_pairs={{0,2},{2,0},{4,6},{6,4},{8,10},{10,8},{12,14},{14,12},{1,3},{3,1},... | collective-permute-start | bytes 221192 | tf_op jit(solution)/shard_map/ppermute | solution.py:15
  8.2 13.5 %collective-permute-start.8 = (bf16[576,2304]{1,0:T(8,128)(2,1)}, bf16[576,2304]{1,0:T(8,128)(2,1)S(1)}, u32[]{:S(2)}, u32[]{:S(2)}) collective-permute-start(bf16[576,2304]{1,0:T(8,128)(2,1)} %own_w_ref.1), channel_id=1, source_target_pairs={{0,1},{1,0},{2,3},{3,2},{4,5},{5,4},{6,7},{7,6},{8,9},{9,8},{10,11... | collective-permute-start | bytes 7962632 | tf_op jit(solution)/shard_map/ppermute | solution.py:15
  8.2 0.8 %copy-start.1 = (bf16[16,1152]{1,0:T(8,128)(2,1)S(1)}, bf16[16,1152]{1,0:T(8,128)(2,1)}, u32[]{:S(2)}) copy-start(bf16[16,1152]{1,0:T(8,128)(2,1)} %q_any.1) | copy-start | bytes 110596
  8.9 0.7 %copy-start.2 = (f32[96]{0:T(128)S(1)}, f32[96]{0:T(128)}, u32[]{:S(2)}) copy-start(f32[96]{0:T(128)} %param.9) | copy-start | bytes 1156
  9.6 0.7 %copy-start.3 = (f32[96]{0:T(128)S(1)}, f32[96]{0:T(128)}, u32[]{:S(2)}) copy-start(f32[96]{0:T(128)} %param.10) | copy-start | bytes 1156
  11.1 8.5 %collective-permute-start.6 = (bf16[16,2304]{1,0:T(8,128)(2,1)S(1)}, bf16[16,2304]{1,0:T(8,128)(2,1)S(1)}, u32[]{:S(2)}, u32[]{:S(2)}) collective-permute-start(bf16[16,2304]{1,0:T(8,128)(2,1)S(1)} %collective-permute-done), channel_id=1, source_target_pairs={{0,12},{2,14},{4,8},{6,10},{8,4},{10,6},{12,0},{14,2},{1,13},{3,15... | collective-permute-start | bytes 221192 | tf_op jit(solution)/shard_map/ppermute | solution.py:15
  14.8 4.7 %collective-permute-start.2 = (bf16[16,2304]{1,0:T(8,128)(2,1)S(1)}, bf16[16,2304]{1,0:T(8,128)(2,1)S(1)}, u32[]{:S(2)}, u32[]{:S(2)}) collective-permute-start(bf16[16,2304]{1,0:T(8,128)(2,1)S(1)} %collective-permute-done), channel_id=1, source_target_pairs={{0,4},{2,6},{4,0},{6,2},{8,12},{10,14},{12,8},{14,10},{1,5},{3,7},... | collective-permute-start | bytes 221192 | tf_op jit(solution)/shard_map/ppermute | solution.py:15
  14.9 4.6 %collective-permute-start.4 = (bf16[16,2304]{1,0:T(8,128)(2,1)S(1)}, bf16[16,2304]{1,0:T(8,128)(2,1)S(1)}, u32[]{:S(2)}, u32[]{:S(2)}) collective-permute-start(bf16[16,2304]{1,0:T(8,128)(2,1)S(1)} %collective-permute-done.3), channel_id=1, source_target_pairs={{0,2},{2,0},{4,6},{6,4},{8,10},{10,8},{12,14},{14,12},{1,3},{3,1},... | collective-permute-start | bytes 221192 | tf_op jit(solution)/shard_map/ppermute | solution.py:15
  19.6 2.1 %copy-start = (bf16[576,2304]{1,0:T(8,128)(2,1)S(1)}, bf16[576,2304]{1,0:T(8,128)(2,1)}, u32[]{:S(2)}) copy-start(bf16[576,2304]{1,0:T(8,128)(2,1)} %own_w_ref.1) | copy-start | bytes 7962628
  19.6 2.1 %collective-permute-start.7 = (bf16[128,2304]{1,0:T(8,128)(2,1)S(1)}, bf16[128,2304]{1,0:T(8,128)(2,1)S(1)}, u32[]{:S(2)}, u32[]{:S(2)}) collective-permute-start(bf16[128,2304]{1,0:T(8,128)(2,1)S(1)} %constant_dynamic-update-slice_fusion.mine_ref), channel_id=1, source_target_pairs={{0,1},{1,0},{2,3},{3,2},{4,5},{5,4},{6,7},{7,6},{8,9},{9,8},{10,11... | collective-permute-start | bytes 1769480 | tf_op jit(solution)/shard_map/ppermute | solution.py:15
